TPU v7x, 32 devices: a whole 2x2x4 slice. The times are simulated.
32 devices in a mesh: group: 1, ctx: 32 (over z, y, x, core).
Axes of the slice: x: 2, y: 2, z: 4, core: 2. Of those that a mesh axis runs over, the one named last changes fastest.
Arguments:
- queries: bfloat16 [2, 64, 128], P('group'), may hold values from -80 to 80
- key_cache: bfloat16 [2, 4096, 512], P('group', 'ctx'), may hold values from -4 to 4
- value_cache: bfloat16 [2, 4096, 512], P('group', 'ctx'), may hold values from -6 to 6
- out_weight: bfloat16 [8192, 4096], P('ctx'), may hold values from -0.125 to 0.125
- hidden_in: bfloat16 [2, 4096], P('group'), may hold values from -45 to 45
- norm_gain: float32 [4096], replicated, may hold values from 0.25 to 1.75
- gate_weight: bfloat16 [32, 4096, 192], P('ctx'), may hold values from -0.09375 to 0.09375
- up_weight: bfloat16 [32, 4096, 192], P('ctx'), may hold values from -0.09375 to 0.09375
- down_weight: bfloat16 [32, 192, 4096], P('ctx'), may hold values from -0.15625 to 0.15625
- routes: int32 [2, 4], P('group'), may hold values from 0 to 3, all different within a row; in each aligned block of 2 rows (0 to 1, 2 to 3, ...) at most 2 rows name the same one
- route_weight: float32 [2, 4], P('group'), may hold values from 0.1 to 1
Outputs:
- mixed: float32 [2, 4096], P('group', 'ctx')
Inputs may be any that keep to these rules, and one draw needn't show every extreme that they name: `routes`: each row names 4 different experts; no expert is named by more than 2 rows, a bound that some block reaches.
All inputs are finite; a program needn't handle non-finite values.
Results may differ from a plain program's by a relative error of at most 0.0035.
Values may be sent and summed in bfloat16 or wider, within the bound.
No kernel may reach another device: no remote copies, remote signals or barrier semaphores. Data moves between devices by JAX's collectives and lax.ppermute only.
A program may use at most 64 MiB of HBM per device.

v0:
```python
import jax
import jax.numpy as jnp
from jax import lax
from jax.sharding import PartitionSpec as P

QUARTERS = 8
eps = 1e-06


def slot_numbers(routes, expert_count):
    flat_routes = routes.reshape(-1)
    onehot = (flat_routes[:, None] == jnp.arange(expert_count, dtype=jnp.int32)[None, :]).astype(
        jnp.int32
    )
    before = jnp.cumsum(onehot, axis=0) - onehot
    return jnp.sum(before * onehot, axis=1)


def body(
    queries,
    key_cache,
    value_cache,
    out_weight,
    hidden_in,
    norm_gain,
    gate_weight,
    up_weight,
    down_weight,
    routes,
    route_weight,
):
    devices = lax.axis_size("ctx")
    my_index = lax.axis_index("ctx")
    seq_count, head_count, head_dim = queries.shape
    kv_heads = key_cache.shape[2] // head_dim
    group_size = head_count // kv_heads
    model_width = hidden_in.shape[1]
    local_len = key_cache.shape[1]
    query_view = queries.reshape(seq_count, kv_heads, group_size, head_dim)
    key_view = key_cache.reshape(seq_count, local_len, kv_heads, head_dim)
    value_view = value_cache.reshape(seq_count, local_len, kv_heads, head_dim)
    scores = jnp.einsum(
        "sgjd,scgd->sgjc", query_view, key_view, preferred_element_type=jnp.float32
    ) * head_dim ** (-0.5)
    row_peak = lax.pmax(jnp.max(scores, axis=-1), "ctx")
    numer = jnp.exp(scores - row_peak[..., None])
    denom_part = jnp.sum(numer, axis=-1)
    partial_value = jnp.einsum(
        "sgjc,scgd->sgjd",
        numer.astype(jnp.bfloat16),
        value_view,
        preferred_element_type=jnp.float32,
    )
    partial_value = partial_value.reshape(seq_count, head_count * head_dim)
    feat_dev = head_count * head_dim // devices
    feat_start = my_index * feat_dev
    summed, denoms = lax.psum((partial_value, denom_part), "ctx")
    attn_mine = lax.dynamic_slice_in_dim(summed, feat_start, feat_dev, 1)
    spread_denoms = jnp.repeat(denoms.reshape(seq_count, head_count), head_dim, axis=1)
    mine_denoms = lax.dynamic_slice_in_dim(spread_denoms, feat_start, feat_dev, 1)
    attended = (attn_mine / mine_denoms).astype(jnp.bfloat16)
    proj_part = jnp.dot(attended, out_weight, preferred_element_type=jnp.float32)
    col_dev = model_width // devices
    col_start = my_index * col_dev
    projected = lax.psum(proj_part, "ctx")
    resid = hidden_in.astype(jnp.float32) + projected
    inverse_rms = lax.rsqrt(jnp.mean(resid * resid, axis=-1, keepdims=True) + eps)
    normed = (resid * inverse_rms * norm_gain).astype(jnp.bfloat16)
    resid_mine = lax.dynamic_slice_in_dim(resid, col_start, col_dev, 1)
    expert_count = devices // QUARTERS
    top_count = routes.shape[1]
    capacity = min(2 * seq_count * top_count // expert_count, seq_count)
    expert = my_index // QUARTERS
    slot_index = slot_numbers(routes, expert_count)
    flat_routes = routes.reshape(-1)
    token_of = jnp.arange(seq_count * top_count, dtype=jnp.int32) // top_count
    matches = (
        (flat_routes[None, :] == expert)
        & (slot_index[None, :] == jnp.arange(capacity, dtype=jnp.int32)[:, None])
    ).astype(jnp.float32)
    owners = (token_of[:, None] == jnp.arange(seq_count, dtype=jnp.int32)[None, :]).astype(
        jnp.float32
    )
    select = jnp.dot(matches, owners, precision=lax.Precision.HIGHEST)
    slot_weight = jnp.dot(matches, route_weight.reshape(-1), precision=lax.Precision.HIGHEST)
    picked_rows = jnp.dot(
        select.astype(jnp.bfloat16), normed, preferred_element_type=jnp.float32
    ).astype(jnp.bfloat16)
    gate_act = jnp.dot(picked_rows, gate_weight[0], preferred_element_type=jnp.float32)
    up_act = jnp.dot(picked_rows, up_weight[0], preferred_element_type=jnp.float32)
    hidden = (jax.nn.silu(gate_act) * up_act).astype(jnp.bfloat16)
    expert_out = (
        jnp.dot(hidden, down_weight[0], preferred_element_type=jnp.float32) * slot_weight[:, None]
    )
    received = lax.all_to_all(
        expert_out.astype(jnp.bfloat16), "ctx", split_axis=1, concat_axis=0, tiled=True
    ).astype(expert_out.dtype)
    quarter_ids = jnp.arange(QUARTERS, dtype=jnp.int32)[None, None, :]
    shard_rows = (routes[:, :, None] * QUARTERS + quarter_ids) * capacity + slot_index.reshape(
        seq_count, top_count
    )[:, :, None]
    moe_mine = jnp.sum(received[shard_rows], axis=(1, 2))
    return resid_mine + moe_mine


def solution(mesh):
    in_specs = (
        P("group", None, None),
        P("group", "ctx", None),
        P("group", "ctx", None),
        P("ctx", None),
        P("group", None),
        P(),
        P("ctx", None, None),
        P("ctx", None, None),
        P("ctx", None, None),
        P("group", None),
        P("group", None),
    )
    out_specs = P("group", "ctx")
    return jax.shard_map(body, mesh=mesh, in_specs=in_specs, out_specs=out_specs, check_vma=False)
```

profile of v0, /device:TPU:0, one launch (start us, length us, event | category | flops | bytes accessed | tf_op | source)
XLA Modules:
  0.0 239.1 jit_solution(7500703949883063939)
XLA Ops:
  6.5 0.0 copy-start
  6.5 1.4 fusion.41
  8.0 42.0 %pmax.7 = f32[2,4,16]{2,1,0:T(4,128)S(1)} all-reduce(f32[2,4,16]{2,1,0:T(4,128)S(1)} %get-tuple-element.7), channel_id=1, replica_groups=mesh['group'=1,'ctx'=32] {'ctx'}, use_global_device_ids=true, to_apply=%region_1.0 | all-reduce | flops 128 | bytes 1024 | tf_op jit(solution)/shard_map/pmax | solution.py:45
  50.0 1.2 fusion.17
  51.2 0.7 copy.38
  51.9 0.0 all-reduce.2.cloned.1.call-update
  51.9 0.8 broadcast_in_dim_reshape.2
  52.7 0.7 broadcast_multiply_fusion
  53.3 0.2 fusion.22
  53.6 0.8 reshape.100
  54.3 0.2 reduce_window_sum.11
  54.5 0.1 add.95
  54.6 0.1 reshape.87
  54.7 40.0 %psum.22 = f32[2,64]{1,0:T(2,128)S(1)} all-reduce(f32[2,64]{1,0:T(2,128)S(1)} %reshape.87), channel_id=1, replica_groups=mesh['group'=1,'ctx'=32] {'ctx'}, use_global_device_ids=true, to_apply=%region_4.0 | all-reduce | flops 128 | bytes 1024 | tf_op jit(solution)/shard_map/psum | solution.py:57
  94.7 0.1 broadcast_bitcast_fusion
  94.8 0.2 convolution_convert_fusion.1
  95.0 0.1 compare_select_fusion
  95.1 0.1 convolution_bitcast_fusion
  95.2 0.1 reshape.93
  95.3 0.1 copy.37
  95.3 76.0 %all-reduce.2.cloned.1.call-done = f32[2,8192]{1,0:T(2,128)} async-done(((f32[2,8192]{1,0:T(2,128)}), f32[2,8192]{1,0:T(2,128)}) %all-reduce.2.cloned.1.call-update) | async-done | bytes 65552 | tf_op jit(solution)/shard_map/psum | solution.py:57
  171.4 1.1 fusion.32
  172.4 41.0 %psum.23 = f32[2,4096]{1,0:T(2,128)S(1)} all-reduce(f32[2,4096]{1,0:T(2,128)S(1)} %fusion.32), channel_id=1, replica_groups=mesh['group'=1,'ctx'=32] {'ctx'}, use_global_device_ids=true, to_apply=%region_5.0 | all-reduce | flops 8192 | bytes 65536 | tf_op jit(solution)/shard_map/psum | solution.py:65
  213.5 0.1 multiply_reduce_fusion
  213.6 0.0 copy-done.2
  213.6 0.2 convolution_convert_fusion
  213.8 1.9 fusion.4
  215.8 3.7 %fusion.6 = bf16[2,32,128]{2,0,1:T(2,128)(2,1)} fusion(bf16[1,192,4096]{2,1,0:T(8,128)(2,1)} %param.19, bf16[2,4096]{1,0:T(2,128)(2,1)S(1)} %convolution_convert_fusion, bf16[1,4096,192]{1,2,0:T(8,128)(2,1)} %param.18, f32[2]{0:T(128)S(1)} %convolution_bitcast_fusion, f32[2,192]{1,0:T(2,128)S(1)} %fusion.4), kind=kOutput, calls=%fused_computation.10 | convolution fusion | flops 6310144 | bytes 3180040 | tf_op jit(solution)/shard_map/dot_general | solution.py:93
  219.5 4.4 %all-to-all-start = ((bf16[2,32,128]{2,0,1:T(2,128)(2,1)}), bf16[2,32,128]{2,0,1:T(2,128)(2,1)S(1)}, u32[]{:S(2)}, u32[]{:S(2)}) async-start(bf16[2,32,128]{2,0,1:T(2,128)(2,1)} %fusion.6), calls=%async_computation | async-start | bytes 32768 | tf_op jit(solution)/shard_map/all_to_all | solution.py:95
  223.9 7.2 %all-to-all-done = bf16[2,32,128]{2,0,1:T(2,128)(2,1)S(1)} async-done(((bf16[2,32,128]{2,0,1:T(2,128)(2,1)}), bf16[2,32,128]{2,0,1:T(2,128)(2,1)S(1)}, u32[]{:S(2)}, u32[]{:S(2)}) %all-to-all-start) | async-done | bytes 16416 | tf_op jit(solution)/shard_map/all_to_all | solution.py:95
  231.1 0.6 gather_fusion
  231.7 0.6 dynamic-slice_add_fusion
  (13 shorter events, 0.1 us)
Async XLA Ops:
  6.5 164.8 %copy-start = (bf16[256,4096]{1,0:T(8,128)(2,1)S(1)}, bf16[256,4096]{1,0:T(8,128)(2,1)}, u32[]{:S(2)}) copy-start(bf16[256,4096]{1,0:T(8,128)(2,1)} %param.14) | copy-start | bytes 6291460
  6.5 164.8 %all-reduce.2.cloned.1.call-start = ((), (), s32[]{:S(2)}) async-start(), calls=%async_computation.1 | async-start | bytes 131072 | tf_op jit(solution)/shard_map/psum | solution.py:57
  50.0 163.5 %copy-start.1 = (bf16[2,4096]{1,0:T(2,128)(2,1)S(1)}, bf16[2,4096]{1,0:T(2,128)(2,1)}, u32[]{:S(2)}) copy-start(bf16[2,4096]{1,0:T(2,128)(2,1)} %param.15) | copy-start | bytes 49156
  50.0 163.6 %copy-start.2 = (f32[4096]{0:T(1024)S(1)}, f32[4096]{0:T(1024)}, u32[]{:S(2)}) copy-start(f32[4096]{0:T(1024)} %param.16) | copy-start | bytes 49156
  219.5 11.6 %all-to-all-start = ((bf16[2,32,128]{2,0,1:T(2,128)(2,1)}), bf16[2,32,128]{2,0,1:T(2,128)(2,1)S(1)}, u32[]{:S(2)}, u32[]{:S(2)}) async-start(bf16[2,32,128]{2,0,1:T(2,128)(2,1)} %fusion.6), calls=%async_computation | async-start | bytes 32768 | tf_op jit(solution)/shard_map/all_to_all | solution.py:95
Sparse Core Ops, SparseCore 0:
  52.0 119.3 all-reduce.1
where the time goes:
time: 240 us; the launch traced here: 239 us
  blocking collectives  123 us (51%)
  waiting for transfers between devices  83.2 us (35%)
  between operations  13.5 us (6%)
  matrix products  9.84 us (4%)
  starting transfers between devices  4.4 us (2%)
  local copies, waits for them, and re-layouts  3.2 us (1%)
    psum x1, waiting for transfers between devices, body(): summed, denoms = lax.psum((partial_value, denom_part), 'ctx')  76 us
    pmax x1, blocking collectives, body(): row_peak = lax.pmax(jnp.max(scores, axis=-1), 'ctx')  42 us
    psum x1, blocking collectives, body(): projected = lax.psum(proj_part, 'ctx')  41 us
    psum x1, blocking collectives, body(): summed, denoms = lax.psum((partial_value, denom_part), 'ctx')  40 us
    all_to_all x1, waiting for transfers between devices, body(): lax.all_to_all(expert_out.astype(jnp.bfloat16), 'ctx', split_axis=1, conc...  7.16 us
  transfers between devices with their start and end apart: 2, of which 2 were waited for; matrix products, arithmetic and copies ran while one was open for 1% of the time, Pallas kernels for 0%

commit v1 on v0

--- a/solution.py
+++ b/solution.py
@@ -1,3 +1,4 @@
+import functools
 import jax
 import jax.numpy as jnp
 from jax import lax
@@ -5,6 +6,18 @@
 
 QUARTERS = 8
 eps = 1e-06
+
+
+def obtain_area(panel, which_axis):
+    n_shards = lax.axis_size(which_axis)
+    view_out = lambda local_out: [(hop_no, hop_no ^ local_out) for hop_no in range(n_shards)]
+    extra = panel
+    for pp in range(n_shards.bit_length() - 1):
+        extra = extra + lax.ppermute(extra, which_axis, view_out(1 << pp))
+    return extra
+
+
+_pair_patch = functools.partial(obtain_area, which_axis="ctx")
 
 
 def slot_numbers(routes, expert_count):
@@ -62,7 +75,7 @@
     proj_part = jnp.dot(attended, out_weight, preferred_element_type=jnp.float32)
     col_dev = model_width // devices
     col_start = my_index * col_dev
-    projected = lax.psum(proj_part, "ctx")
+    projected = _pair_patch(proj_part)
     resid = hidden_in.astype(jnp.float32) + projected
     inverse_rms = lax.rsqrt(jnp.mean(resid * resid, axis=-1, keepdims=True) + eps)
     normed = (resid * inverse_rms * norm_gain).astype(jnp.bfloat16)

time: 240 us -> 218 us (0.908)
  blocking collectives: 123 us -> 82 us
  waiting for transfers between devices: 83.2 us -> 95.1 us
  starting transfers between devices: 4.4 us -> 12.7 us
    psum x1 -> x0, blocking collectives: 41 us -> none  [body(): projected = lax.psum(proj_part, 'ctx')]
    ppermute x0 -> x5, waiting for transfers between devices: none -> 10.6 us  [obtain_area(): extra = extra + lax.ppermute(extra, which_axis, view_out(1 << pp))]
    ppermute x0 -> x5, starting transfers between devices: none -> 8.26 us  [obtain_area(): extra = extra + lax.ppermute(extra, which_axis, view_out(1 << pp))]
  transfers between devices with their start and end apart: 2 -> 7, of which waited for: 2 -> 7; matrix products, arithmetic and copies ran while one was open for 1% -> 1% of each run, Pallas kernels for 0% -> 0%
where the time goes in v1:
time: 218 us
  waiting for transfers between devices  95.1 us (44%)
  blocking collectives  82 us (38%)
  between operations  13.5 us (6%)
  starting transfers between devices  12.7 us (6%)
  matrix products  9.81 us (4%)
  local copies, waits for them, and re-layouts  2.51 us (1%)
    psum x1, waiting for transfers between devices, body(): summed, denoms = lax.psum((partial_value, denom_part), 'ctx')  77.3 us
    pmax x1, blocking collectives, body(): row_peak = lax.pmax(jnp.max(scores, axis=-1), 'ctx')  42 us
    psum x1, blocking collectives, body(): summed, denoms = lax.psum((partial_value, denom_part), 'ctx')  39.9 us
    ppermute x5, waiting for transfers between devices, obtain_area(): extra = extra + lax.ppermute(extra, which_axis, view_out(1 << pp))  10.6 us
    ppermute x5, starting transfers between devices, obtain_area(): extra = extra + lax.ppermute(extra, which_axis, view_out(1 << pp))  8.26 us
    all_to_all x1, waiting for transfers between devices, body(): lax.all_to_all(expert_out.astype(jnp.bfloat16), 'ctx', split_axis=1, conc...  7.16 us
    all_to_all x1, starting transfers between devices, body(): lax.all_to_all(expert_out.astype(jnp.bfloat16), 'ctx', split_axis=1, conc...  4.47 us
  transfers between devices with their start and end apart: 7, of which 7 were waited for; matrix products, arithmetic and copies ran while one was open for 1% of the time, Pallas kernels for 0%

profile of v1, /device:TPU:0, one launch (start us, length us, event | category | flops | bytes accessed | tf_op | source)
XLA Modules:
  0.0 217.5 jit_solution(10226316898114296161)
XLA Ops:
  6.5 1.4 fusion.41
  8.0 42.0 %pmax.7 = f32[2,4,16]{2,1,0:T(4,128)S(1)} all-reduce(f32[2,4,16]{2,1,0:T(4,128)S(1)} %get-tuple-element.7), channel_id=1, replica_groups=mesh['group'=1,'ctx'=32] {'ctx'}, use_global_device_ids=true, to_apply=%region_1.0 | all-reduce | flops 128 | bytes 1024 | tf_op jit(solution)/shard_map/pmax | solution.py:58
  50.0 1.2 fusion.17
  51.2 0.7 copy.38
  51.9 0.2 fusion.22
  52.0 0.8 broadcast_in_dim_reshape.2
  52.8 0.7 broadcast_multiply_fusion
  53.6 39.9 %psum.15 = f32[2,64]{1,0:T(2,128)S(1)} all-reduce(f32[2,64]{1,0:T(2,128)S(1)} %reshape.87), channel_id=1, replica_groups=mesh['group'=1,'ctx'=32] {'ctx'}, use_global_device_ids=true, to_apply=%region_4.0 | all-reduce | flops 128 | bytes 1024 | tf_op jit(solution)/shard_map/psum | solution.py:70
  93.6 0.2 reduce_window_sum.11
  94.0 77.3 %all-reduce.2.cloned.1.call-done = f32[2,8192]{1,0:T(2,128)} async-done(((f32[2,8192]{1,0:T(2,128)}), f32[2,8192]{1,0:T(2,128)}) %all-reduce.2.cloned.1.call-update) | async-done | bytes 65552 | tf_op jit(solution)/shard_map/psum | solution.py:70
  171.3 1.1 fusion.32
  172.3 1.7 collective-permute-start
  174.1 0.8 collective-permute-done
  174.9 1.5 collective-permute-start.1
  176.5 2.4 %collective-permute-done.1 = f32[2,4096]{1,0:T(2,128)S(1)} collective-permute-done((f32[2,4096]{1,0:T(2,128)S(1)}, f32[2,4096]{1,0:T(2,128)S(1)}, u32[]{:S(2)}, u32[]{:S(2)}) %collective-permute-start.1) | collective-permute-done | bytes 32800 | tf_op jit(solution)/shard_map/ppermute | solution.py:16
  178.9 1.5 collective-permute-start.2
  180.5 2.4 %collective-permute-done.2 = f32[2,4096]{1,0:T(2,128)S(1)} collective-permute-done((f32[2,4096]{1,0:T(2,128)S(1)}, f32[2,4096]{1,0:T(2,128)S(1)}, u32[]{:S(2)}, u32[]{:S(2)}) %collective-permute-start.2) | collective-permute-done | bytes 32800 | tf_op jit(solution)/shard_map/ppermute | solution.py:16
  182.9 1.6 collective-permute-start.3
  184.5 0.2 convolution_convert_fusion.1
  184.8 2.1 collective-permute-done.3
  186.9 1.9 collective-permute-start.4
  188.8 0.1 convolution_bitcast_fusion
  188.9 0.1 reshape.93
  189.0 2.8 %collective-permute-done.4 = f32[2,4096]{1,0:T(2,128)S(1)} collective-permute-done((f32[2,4096]{1,0:T(2,128)S(1)}, f32[2,4096]{1,0:T(2,128)S(1)}, u32[]{:S(2)}, u32[]{:S(2)}) %collective-permute-start.4) | collective-permute-done | bytes 32800 | tf_op jit(solution)/shard_map/ppermute | solution.py:16
  191.8 0.1 multiply_reduce_fusion
  192.0 0.2 convolution_convert_fusion
  192.2 1.9 fusion.4
  194.1 3.7 %fusion.6 = bf16[2,32,128]{2,0,1:T(2,128)(2,1)} fusion(bf16[1,192,4096]{2,1,0:T(8,128)(2,1)} %param.19, bf16[2,4096]{1,0:T(2,128)(2,1)S(1)} %convolution_convert_fusion, bf16[1,4096,192]{1,2,0:T(8,128)(2,1)} %param.18, f32[2]{0:T(128)S(1)} %convolution_bitcast_fusion, f32[2,192]{1,0:T(2,128)S(1)} %fusion.4), kind=kOutput, calls=%fused_computation.10 | convolution fusion | flops 6310144 | bytes 3180040 | tf_op jit(solution)/shard_map/dot_general | solution.py:106
  197.8 4.5 %all-to-all-start = ((bf16[2,32,128]{2,0,1:T(2,128)(2,1)}), bf16[2,32,128]{2,0,1:T(2,128)(2,1)S(1)}, u32[]{:S(2)}, u32[]{:S(2)}) async-start(bf16[2,32,128]{2,0,1:T(2,128)(2,1)} %fusion.6), calls=%async_computation | async-start | bytes 32768 | tf_op jit(solution)/shard_map/all_to_all | solution.py:108
  202.3 7.2 %all-to-all-done = bf16[2,32,128]{2,0,1:T(2,128)(2,1)S(1)} async-done(((bf16[2,32,128]{2,0,1:T(2,128)(2,1)}), bf16[2,32,128]{2,0,1:T(2,128)(2,1)S(1)}, u32[]{:S(2)}, u32[]{:S(2)}) %all-to-all-start) | async-done | bytes 16416 | tf_op jit(solution)/shard_map/all_to_all | solution.py:108
  209.5 0.6 gather_fusion
  210.1 0.6 dynamic-slice_add_fusion
  (28 shorter events, 0.6 us)
Async XLA Ops:
  6.5 164.7 %copy-start = (bf16[256,4096]{1,0:T(8,128)(2,1)S(1)}, bf16[256,4096]{1,0:T(8,128)(2,1)}, u32[]{:S(2)}) copy-start(bf16[256,4096]{1,0:T(8,128)(2,1)} %param.14) | copy-start | bytes 6291460
  6.5 164.7 %all-reduce.2.cloned.1.call-start = ((), (), s32[]{:S(2)}) async-start(), calls=%async_computation.1 | async-start | bytes 131072 | tf_op jit(solution)/shard_map/psum | solution.py:70
  51.2 133.6 %copy-start.3 = (f32[2,4]{1,0:T(2,128)S(1)}, f32[2,4]{1,0:T(2,128)}, u32[]{:S(2)}) copy-start(f32[2,4]{1,0:T(2,128)} %param.21) | copy-start | bytes 100
  51.2 140.7 %copy-start.1 = (bf16[2,4096]{1,0:T(2,128)(2,1)S(1)}, bf16[2,4096]{1,0:T(2,128)(2,1)}, u32[]{:S(2)}) copy-start(bf16[2,4096]{1,0:T(2,128)(2,1)} %param.15) | copy-start | bytes 49156
  51.8 140.1 %copy-start.2 = (f32[4096]{0:T(1024)S(1)}, f32[4096]{0:T(1024)}, u32[]{:S(2)}) copy-start(f32[4096]{0:T(1024)} %param.16) | copy-start | bytes 49156
  172.3 2.6 %collective-permute-start = (f32[2,4096]{1,0:T(2,128)S(1)}, f32[2,4096]{1,0:T(2,128)S(1)}, u32[]{:S(2)}, u32[]{:S(2)}) collective-permute-start(f32[2,4096]{1,0:T(2,128)S(1)} %fusion.32), channel_id=1, source_target_pairs={{0,1},{1,0},{2,3},{3,2},{4,5},{5,4},{6,7},{7,6},{8,9},{9,8},{10,11... | collective-permute-start | bytes 98312 | tf_op jit(solution)/shard_map/ppermute | solution.py:16
  174.9 4.0 %collective-permute-start.1 = (f32[2,4096]{1,0:T(2,128)S(1)}, f32[2,4096]{1,0:T(2,128)S(1)}, u32[]{:S(2)}, u32[]{:S(2)}) collective-permute-start(f32[2,4096]{1,0:T(2,128)S(1)} %add.101), channel_id=1, source_target_pairs={{0,2},{1,3},{2,0},{3,1},{4,6},{5,7},{6,4},{7,5},{8,10},{9,11},{10,... | collective-permute-start | bytes 98312 | tf_op jit(solution)/shard_map/ppermute | solution.py:16
  178.9 4.0 %collective-permute-start.2 = (f32[2,4096]{1,0:T(2,128)S(1)}, f32[2,4096]{1,0:T(2,128)S(1)}, u32[]{:S(2)}, u32[]{:S(2)}) collective-permute-start(f32[2,4096]{1,0:T(2,128)S(1)} %add.102), channel_id=1, source_target_pairs={{0,4},{1,5},{2,6},{3,7},{4,0},{5,1},{6,2},{7,3},{8,12},{9,13},{10,... | collective-permute-start | bytes 98312 | tf_op jit(solution)/shard_map/ppermute | solution.py:16
  182.9 4.0 %collective-permute-start.3 = (f32[2,4096]{1,0:T(2,128)S(1)}, f32[2,4096]{1,0:T(2,128)S(1)}, u32[]{:S(2)}, u32[]{:S(2)}) collective-permute-start(f32[2,4096]{1,0:T(2,128)S(1)} %add.103), channel_id=1, source_target_pairs={{0,8},{1,9},{2,10},{3,11},{4,12},{5,13},{6,14},{7,15},{8,0},{9,1},... | collective-permute-start | bytes 98312 | tf_op jit(solution)/shard_map/ppermute | solution.py:16
  186.9 4.9 %collective-permute-start.4 = (f32[2,4096]{1,0:T(2,128)S(1)}, f32[2,4096]{1,0:T(2,128)S(1)}, u32[]{:S(2)}, u32[]{:S(2)}) collective-permute-start(f32[2,4096]{1,0:T(2,128)S(1)} %add.104), channel_id=1, source_target_pairs={{0,16},{1,17},{2,18},{3,19},{4,20},{5,21},{6,22},{7,23},{8,24},{9,... | collective-permute-start | bytes 98312 | tf_op jit(solution)/shard_map/ppermute | solution.py:16
  197.8 11.7 %all-to-all-start = ((bf16[2,32,128]{2,0,1:T(2,128)(2,1)}), bf16[2,32,128]{2,0,1:T(2,128)(2,1)S(1)}, u32[]{:S(2)}, u32[]{:S(2)}) async-start(bf16[2,32,128]{2,0,1:T(2,128)(2,1)} %fusion.6), calls=%async_computation | async-start | bytes 32768 | tf_op jit(solution)/shard_map/all_to_all | solution.py:108
Sparse Core Ops, SparseCore 0:
  52.0 119.2 all-reduce.1
